TPU v7x, 32 devices: a whole 2x2x4 slice. The times are simulated.
32 devices in a mesh: ctx: 8 (over y, x, core), tp: 4 (over z).
Axes of the slice: x: 2, y: 2, z: 4, core: 2. Of those that a mesh axis runs over, the one named last changes fastest.
Arguments:
- queries: bfloat16 [2048, 8192], P('ctx', 'tp'), may hold values from -8 to 8
- keys: bfloat16 [2048, 1024], P('ctx'), may hold values from -6 to 6
- values: bfloat16 [2048, 1024], P('ctx'), may hold values from -6 to 6
Outputs:
- attended: bfloat16 [2048, 8192], P('ctx', 'tp')
All inputs are finite; a program needn't handle non-finite values.
Results may differ from a plain program's by a relative error of at most 0.0032.
Values may be sent and summed in bfloat16 or wider, within the bound.
A program may use at most 64 MiB of HBM per device.

v0:
```python
import functools
import math

import jax
import jax.numpy as jnp
from jax import lax
from jax.experimental import pallas as pl
from jax.experimental.pallas import tpu as pltpu
from jax.sharding import PartitionSpec as P

HEADS = 64
KV_HEADS = 8
HEAD_DIM = 128
LANES = 128
MASKED = -1e30
CHUNK = 8
DEPTH = 1
ROUTED = 1
EXP2_SCALE = HEAD_DIM ** -0.5 * math.log2(math.e)


def attend_heads(q_v, kv, acc, peak, heads, kv_head, blocks, masked, first):
    k = jnp.concatenate([kv[b, kv_head, 0] for b in blocks], 0)
    v = jnp.concatenate([kv[b, kv_head, 1] for b in blocks], 0)
    v = jnp.concatenate([v, jnp.ones((v.shape[0], LANES), v.dtype)], 1)
    rows, count = q_v.shape[0], k.shape[0]

    def score(h):
        q = q_v[:, pl.ds(pl.multiple_of(h * HEAD_DIM, HEAD_DIM), HEAD_DIM)]
        return lax.dot_general(q, k, (((1,), (1,)), ((), ())), preferred_element_type=jnp.float32)

    def fold(h, s):
        if masked:
            row = lax.broadcasted_iota(jnp.int32, s.shape, 0)
            col = lax.broadcasted_iota(jnp.int32, s.shape, 1)
            s = jnp.where(col <= row, s, MASKED)
        top = jnp.broadcast_to(jnp.max(s, axis=1, keepdims=True), (rows, LANES))
        if not first:
            before = peak[h]
            top = jnp.maximum(before, top)
        peak[h] = top
        wide = jnp.concatenate([top] * (count // LANES), 1)
        w = jnp.exp2((s - wide) * EXP2_SCALE).astype(jnp.bfloat16)
        new = jnp.dot(w, v, preferred_element_type=jnp.float32)
        if not first:
            shrink = jnp.exp2((before - top) * EXP2_SCALE)
            new = acc[h] * jnp.concatenate([shrink, shrink], 1) + new
        acc[h] = new

    ahead = [score(h) for h in heads[:DEPTH]]
    for i, h in enumerate(heads):
        if i + DEPTH < len(heads):
            ahead.append(score(heads[i + DEPTH]))
        fold(h, ahead.pop(0))


def kernel(nc, per_dev, group, kv_dev, q_hbm, k_hbm, v_hbm, o_ref,
           q_v, kv, acc, peak, loc_sem, send_sem, fwd_sem, far_sem, recv_sem):
    c = lax.axis_index("ctx")
    tp = lax.axis_index("tp")
    odd = lax.rem(c, 2)
    pair = c // 2
    partner = c + 1 - 2 * odd
    shared = per_dev // kv_dev
    chunk = min(CHUNK, shared)
    square = nc == 8 and kv_dev == 2
    base = tp * per_dev // group

    loads = []
    for g in range(kv_dev):
        cols = pl.ds(pl.multiple_of((base + g) * HEAD_DIM, HEAD_DIM), HEAD_DIM)
        loads.append([
            pltpu.make_async_copy(ref.at[:, cols], kv.at[c, g, i], loc_sem.at[2 * g + i])
            for i, ref in enumerate((k_hbm, v_hbm))])
        for load in loads[g]:
            load.start()
    load_q = pltpu.make_async_copy(q_hbm, q_v, loc_sem.at[2 * kv_dev])
    load_q.start()

    barrier = pltpu.get_barrier_semaphore()
    pl.semaphore_signal(barrier, inc=1, device_id={"ctx": partner})
    for i in range(1, nc // 2):
        pl.semaphore_signal(barrier, inc=1, device_id={"ctx": lax.rem(c + 2 * i, nc)})
    pl.semaphore_wait(barrier, nc // 2)

    def copy_to(b, g, target, sem):
        return pltpu.make_async_remote_copy(
            src_ref=kv.at[b, g], dst_ref=kv.at[b, g], send_sem=sem, recv_sem=recv_sem.at[b, g],
            device_id={"ctx": target})

    for load in sum(loads, []):
        load.wait()
    sends, late = [], []
    for g in range(kv_dev):
        sends.append((odd == 0, copy_to(c, g, partner, send_sem.at[0, g])))
        if square:
            beside = copy_to(c, g, lax.rem(c + 2, nc), send_sem.at[1, g])
            sends.append((lax.rem(pair, 2) == 0, beside))
            if g >= ROUTED:
                late.append(beside)
            first = kv_dev - 1 - g
            other = lax.select(pair == 0, first, g)
            sends.append((pair < 2, copy_to(c, other, lax.rem(c + 4, nc), send_sem.at[2, g])))
        else:
            for i in range(1, nc // 2):
                sends.append((c + 2 * i < nc, copy_to(c, g, lax.rem(c + 2 * i, nc), send_sem.at[i, g])))
    for wanted, copy in sends:
        pl.when(wanted)(copy.start)
    load_q.wait()

    def item(t):
        if not square:
            return pair - 1 - t // kv_dev, lax.rem(t, kv_dev)
        third = (lax.select(t < 4, 2 - lax.rem(t, 2), 0), lax.select(t < 4, t // 2, t - 4))
        second = (t // 2, lax.rem((t + 1) // 2 + 1, 2))
        return (lax.select(pair == 3, third[0], lax.select(pair == 2, second[0], 0)),
                lax.select(pair == 3, third[1], lax.select(pair == 2, second[1], t)))

    def onward(p, g):
        mine = 2 * p + odd
        up = ((pair == 1) & (g == 0)) | ((pair == 2) & (p == 0) & (g == 1))
        back = (pair == 3) & (p == 1) & (g < ROUTED)
        target = lax.select(pair == 3, 4 + odd, 6 + odd)
        return up | back, copy_to(mine, g, target, far_sem.at[p, g])

    def pull(t):
        p, g = item(t)
        copy = copy_to(2 * p + odd, g, partner, fwd_sem.at[p, g])
        copy.wait_recv()
        if square:
            wanted, far = onward(p, g)
            pl.when(wanted)(far.start)
        copy.start()

    def sweep(blocks, kv_head, masked, first):
        def body(n, carry):
            heads = [n * chunk + i for i in range(chunk)]
            g = n * chunk // shared if kv_head is None else kv_head
            attend_heads(q_v, kv, acc, peak, heads, g, blocks, masked, first)
            return carry
        return body

    def finish(g, carry):
        for i in range(shared):
            h = g * shared + i
            out = acc[h, :, :LANES] / acc[h, :, LANES:]
            o_ref[:, pl.ds(pl.multiple_of(h * HEAD_DIM, HEAD_DIM), HEAD_DIM)] = out.astype(o_ref.dtype)
        return carry

    chunks = per_dev // chunk
    steps = pair * kv_dev
    lax.fori_loop(0, chunks, sweep([c], None, True, True), 0)

    if square:
        for copy in late:
            pl.when(pair == 1)(copy.start)

    def first_pulls():
        pull(0)
        if square:
            pl.when(pair == 3)(functools.partial(pull, 1))

    @pl.when(odd == 1)
    def _():
        for g in range(kv_dev):
            copy_to(c - 1, g, partner, send_sem.at[0, g]).wait_recv()
        work = sweep([c - 1], None, False, False)

        def body(n, carry):
            pl.when((n == chunks // 2) & (pair > 0))(first_pulls)
            return work(n, carry)

        lax.fori_loop(0, chunks, body, 0)

    pl.when((odd == 0) & (pair > 0))(first_pulls)

    def step(t, carry):
        p, g = item(t)
        copy_to(2 * p + 1 - odd, g, partner, fwd_sem.at[p, g]).wait_recv()
        body = sweep([2 * p, 2 * p + 1], g, False, False)

        done = (pair == 3) & (t == 0) if square else False

        @pl.when((t + 1 < steps) & jnp.logical_not(done))
        def _():
            pull(t + 1)

        per_head = shared // chunk
        lax.fori_loop(g * per_head, (g + 1) * per_head, body, 0)

        @pl.when(t >= steps - kv_dev)
        def _():
            finish(g, 0)
        return carry

    lax.fori_loop(0, steps, step, 0)

    @pl.when(pair == 0)
    def _():
        lax.fori_loop(0, kv_dev, finish, 0)

    def drain(t, carry):
        p, g = item(t)
        copy_to(2 * p + odd, g, partner, fwd_sem.at[p, g]).wait_send()
        if square:
            wanted, far = onward(p, g)
            pl.when(wanted)(far.wait_send)
        return carry

    lax.fori_loop(0, steps, drain, 0)
    for wanted, copy in sends:
        pl.when(wanted)(copy.wait_send)
    for copy in late:
        pl.when(pair == 1)(copy.wait_send)


def solution(mesh):
    nc = mesh.shape["ctx"]

    def step(queries, keys, values):
        rows, width = queries.shape
        per_dev = width // HEAD_DIM
        group = HEADS // KV_HEADS
        kv_dev = per_dev // min(group, per_dev)
        any_space = pl.BlockSpec(memory_space=pltpu.HBM)
        return pl.pallas_call(
            functools.partial(kernel, nc, per_dev, group, kv_dev),
            out_shape=pltpu.VMEM((rows, width), jnp.bfloat16),
            in_specs=[any_space] * 3,
            out_specs=pl.BlockSpec(memory_space=pltpu.VMEM),
            scratch_shapes=[
                pltpu.VMEM((rows, width), jnp.bfloat16),
                pltpu.VMEM((nc, kv_dev, 2, rows, HEAD_DIM), jnp.bfloat16),
                pltpu.VMEM((per_dev, rows, 2 * LANES), jnp.float32),
                pltpu.VMEM((per_dev, rows, LANES), jnp.float32),
                pltpu.SemaphoreType.DMA((2 * kv_dev + 1,)),
                pltpu.SemaphoreType.DMA((nc // 2, kv_dev)),
                pltpu.SemaphoreType.DMA((nc // 2, kv_dev)),
                pltpu.SemaphoreType.DMA((nc // 2, kv_dev)),
                pltpu.SemaphoreType.DMA((nc, kv_dev)),
            ],
            compiler_params=pltpu.CompilerParams(
                collective_id=0, has_side_effects=True, vmem_limit_bytes=60 * 1024 * 1024),
        )(queries, keys, values)

    return jax.shard_map(
        step, mesh=mesh,
        in_specs=(P("ctx", "tp"), P("ctx", None), P("ctx", None)),
        out_specs=P("ctx", "tp"), check_vma=False)
```

profile of v0, /device:TPU:29, one launch (start us, length us, event | category | flops | bytes accessed | tf_op | source)
XLA Modules:
  0.0 20.1 jit_solution(11870748415512226772)
XLA Ops:
  0.0 19.1 %shard_map.37 = bf16[256,2048]{1,0:T(8,128)(2,1)S(1)} custom-call(bf16[256,2048]{1,0:T(8,128)(2,1)} %q_hbm.1, bf16[256,1024]{1,0:T(8,128)(2,1)} %k_hbm.1, bf16[256,1024]{1,0:T(8,128)(2,1)} %v_hbm.1), custom_call_target="tpu_custom_call" | custom-call | tf_op jit(solution)/shard_map/pallas_call | solution.py:226
  19.1 1.0 %copy.5 = bf16[256,2048]{1,0:T(8,128)(2,1)} copy(bf16[256,2048]{1,0:T(8,128)(2,1)S(1)} %shard_map.37) | data formatting | bytes 2097152
where the time goes:
time: 20.3 us; the launch traced here: 20.1 us
  Pallas kernels  19.1 us (94%)
  local copies, waits for them, and re-layouts  0.97 us (5%)
    pallas_call x1, Pallas kernels, step(): pl.pallas_call(functools.partial(kernel, nc, per_dev, group, kv_dev), out...  19.1 us
    unnamed x1, local copies, waits for them, and re-layouts  0.97 us

commit v1 on v0

--- a/solution.py
+++ b/solution.py
@@ -214,6 +214,302 @@
         pl.when(pair == 1)(copy.wait_send)
 
 
+AHEAD = 4
+LAG = 4
+HOLD = 2
+RING = 8
+SUMS = 16
+
+
+def paired_kernel(shared, q_hbm, k_hbm, v_hbm, o_ref, q_raw, q_t, kv, other, acc, peak, shrink,
+                  ring, v_t, stage, load_sem, pair_sem, send_sem, relay_sem, recv_sem, out_sem):
+    c = lax.axis_index("ctx")
+    tp = lax.axis_index("tp")
+    o = lax.rem(c, 2)
+    chip = c // 2
+    partner = c + 1 - 2 * o
+    rows = q_raw.shape[1]
+    half = rows // 2
+    span = shared * HEAD_DIM
+    tiles = 2 * shared
+    f32, bf16 = jnp.float32, jnp.bfloat16
+
+    def head_cols(g, width):
+        return pl.ds(pl.multiple_of(g * width, width), width)
+
+    loads = []
+    for h in range(2):
+        for i, ref in enumerate((k_hbm, v_hbm)):
+            for n, (g, dst) in enumerate(((o, kv.at[c, h, i]), (1 - o, other.at[h, i]))):
+                src = ref.at[pl.ds(h * half, half), head_cols(2 * tp + g, HEAD_DIM)]
+                loads.append(pltpu.make_async_copy(src, dst, load_sem.at[4 * h + 2 * i + n]))
+    for load in loads:
+        load.start()
+    load_q = pltpu.make_async_copy(q_hbm.at[:, head_cols(o, span)], q_raw.at[1], load_sem.at[8])
+    load_q.start()
+
+    barrier = pltpu.get_barrier_semaphore()
+    beside = 2 * (chip + 1 - 2 * lax.rem(chip, 2))
+    across = 2 * lax.rem(chip + 2, 4)
+    for target in (partner, beside, beside + 1, across, across + 1):
+        pl.semaphore_signal(barrier, inc=1, device_id={"ctx": target})
+    v_t[...] = jnp.ones(v_t.shape, bf16)
+    pl.semaphore_wait(barrier, 5)
+
+    def remote(src, dst, send, recv, target):
+        return pltpu.make_async_remote_copy(
+            src_ref=src, dst_ref=dst, send_sem=send, recv_sem=recv, device_id={"ctx": target})
+
+    def piece(b, h, send, target):
+        return remote(kv.at[b, h], kv.at[b, h], send, recv_sem.at[b, h], target)
+
+    give_q = remote(q_hbm.at[:, head_cols(1 - o, span)], q_raw.at[0], pair_sem.at[0], pair_sem.at[1], partner)
+    give_kv = remote(other, kv.at[c], pair_sem.at[2], pair_sem.at[3], partner)
+    give_q.start()
+    for load in loads:
+        load.wait()
+    sends = []
+    for n, (wanted, base, flip) in enumerate((
+            ((chip == 0) | (chip == 2), beside, 0), (chip < 2, across, 1))):
+        for k, (h, swap) in enumerate(((0, 0), (0, 1), (1, 0), (1, 1))):
+            sem = send_sem.at[n, k]
+            same = piece(c, h, sem, base + o)
+            cross = remote(other.at[h], kv.at[c, h], sem, recv_sem.at[c, h], base + 1 - o)
+            if flip:
+                first, then = (same, cross), (cross, same)
+                sends.append((wanted & (chip == 1), first[swap]))
+                sends.append((wanted & (chip == 0), then[swap]))
+            else:
+                sends.append((wanted, (same, cross)[swap]))
+    for wanted, copy in sends:
+        pl.when(wanted)(copy.start)
+    give_kv.start()
+
+    def prepare(slot):
+        for h in range(shared):
+            x = q_raw[slot, :, h * HEAD_DIM:(h + 1) * HEAD_DIM].astype(f32) * EXP2_SCALE
+            x = x.T
+            top = x.astype(bf16)
+            low = (x - top.astype(f32)).astype(bf16)
+            for s in range(2):
+                cols = slice(s * half, (s + 1) * half)
+                q_t[slot * shared + h, s, :HEAD_DIM] = top[:, cols]
+                q_t[slot * shared + h, s, HEAD_DIM:] = low[:, cols]
+
+    def turn(slot, b1, h1, b2, h2):
+        for s, (b, h) in enumerate(((b1, h1), (b2, h2))):
+            v_t[slot, s, :HEAD_DIM] = kv[b, h, 1].astype(f32).T.astype(bf16)
+
+    def bands(x):
+        return x.reshape(x.shape[0] // 8, 8, rows)
+
+    def pipeline(*accs):
+        accs = iter(accs)
+        s_acc = [[[next(accs) for _ in range(2)] for _ in range(2)] for _ in range(2)]
+        o_acc = [[[next(accs) for _ in range(2)] for _ in range(2)] for _ in range(2)]
+
+        def unit(i):
+            return i % 2, i // 2 % 2
+
+        def score(i, t, keys):
+            m, d = unit(i)
+            q = jnp.concatenate([q_t[t, 0], q_t[t, 1]], 1)
+            pltpu.matmul_push_rhs(q, staging_register=0, mxu_index=m)
+            for s, (b, h) in enumerate(keys):
+                k = kv[b, h, 0]
+                pltpu.matmul_acc_lhs(s_acc[m][d][s], jnp.concatenate([k, k], 1),
+                                     load_staged_rhs=None if s else 0)
+
+        def collect(i, t, masked, first):
+            m, d = unit(i)
+            top = None
+            for s in range(2):
+                x = pltpu.matmul_pop(s_acc[m][d][s])
+                if masked:
+                    key = lax.broadcasted_iota(jnp.int32, x.shape, 0) + s * half
+                    row = lax.broadcasted_iota(jnp.int32, x.shape, 1)
+                    x = jnp.where(key <= row, x, MASKED)
+                ring[i % RING, s * half:(s + 1) * half] = x
+                most = jnp.max(bands(x), 0)
+                top = most if top is None else jnp.maximum(top, most)
+            top = jnp.broadcast_to(jnp.max(top, 0, keepdims=True), (8, rows))
+            if not first:
+                before = peak[t]
+                top = jnp.maximum(before, top)
+                shrink[t] = jnp.exp2(before - top)
+            peak[t] = top
+
+        def weigh(i, t, slot):
+            m, d = unit(i)
+            p = jnp.exp2(bands(ring[i % RING]) - peak[t][None]).reshape(rows, rows).astype(bf16)
+            v = jnp.concatenate([v_t[slot, 0], v_t[slot, 1]], 1)
+            pltpu.matmul_push_rhs(p, staging_register=1, mxu_index=m)
+            pltpu.matmul_acc_lhs(o_acc[m][d][0], v[:HEAD_DIM], load_staged_rhs=1)
+            pltpu.matmul_acc_lhs(o_acc[m][d][1], v[HEAD_DIM:])
+
+        def add(i, t, first):
+            m, d = unit(i)
+            new = pltpu.matmul_pop(o_acc[m][d][0])
+            total = pltpu.matmul_pop(o_acc[m][d][1])[:8]
+            if not first:
+                scale = shrink[t]
+                new = (bands(acc[t, :HEAD_DIM]) * scale[None]).reshape(HEAD_DIM, rows) + new
+                total = acc[t, HEAD_DIM:] * scale + total
+            acc[t, :HEAD_DIM] = new
+            acc[t, HEAD_DIM:] = total
+
+        pairs = lambda b: ((b, 0), (b, 1))
+        late = o * shared
+        jobs = []
+        for h in range(shared):
+            jobs.append((shared + h, pairs(c), 0, True, True))
+        for h in range(shared):
+            jobs.append((h, pairs(partner), 1, True, True))
+        for h in range(shared):
+            jobs.append((late + h, pairs(2 * chip), o, False, False))
+
+        load_q.wait()
+        prepare(1)
+        turn(0, c, 0, c, 1)
+
+        def meet():
+            give_kv.wait_recv()
+            give_q.wait_recv()
+            prepare(0)
+            turn(1, partner, 0, partner, 1)
+
+        def start(i):
+            if i == shared:
+                meet()
+            score(i, jobs[i][0], jobs[i][1])
+
+        count = len(jobs)
+        for i in range(AHEAD):
+            start(i)
+        for j in range(count + LAG + HOLD):
+            k = j - LAG
+            if 0 <= k - HOLD:
+                add(k - HOLD, jobs[k - HOLD][0], jobs[k - HOLD][4])
+            if 0 <= k < count:
+                weigh(k, jobs[k][0], jobs[k][2])
+            if j < count:
+                collect(j, jobs[j][0], jobs[j][3], jobs[j][4])
+            if j + AHEAD < count:
+                start(j + AHEAD)
+
+        for t in range(tiles - LAG - HOLD, tiles):
+            shrink[t] = jnp.ones((8, rows), f32)
+        for t in range(tiles - LAG, tiles):
+            ring[t % RING] = jnp.full((rows, rows), MASKED, f32)
+
+        def plan(r):
+            e = lax.rem(r + o, 2)
+            early = r < lax.select(chip == 3, 4, 2)
+            b1 = lax.select(chip == 1, o, lax.select(chip == 2, lax.select(early, 1 - o, 2),
+                                                     lax.select(early, 2 + e, 0)))
+            b2 = lax.select(chip == 1, 1 - o, lax.select(chip == 2, lax.select(early, o, 3),
+                                                         lax.select(early, 4 + e, 1)))
+            h = lax.select(chip == 3, lax.select(early, r // 2, r - 4), lax.rem(r, 2))
+            target = 2 * lax.select(chip == 3, 2, 3) + o
+            return b1, b2, h, early, piece(b1, h, relay_sem.at[r], target)
+
+        def sweep(r, carry):
+            b1, b2, h, early, onward = plan(r)
+            onward.wait_recv()
+            pl.when(early)(onward.start)
+            piece(b2, h, relay_sem.at[r], partner).wait_recv()
+            slot = lax.rem(r, 2)
+            turn(slot, b1, h, b2, h)
+            keys = ((b1, h), (b2, h))
+            for i in range(AHEAD):
+                score(i, i, keys)
+            for j in range(tiles):
+                k = (j - LAG) % tiles
+                n = (j - LAG - HOLD) % tiles
+                add(n, n, False)
+                weigh(k, k, slot if j >= LAG else 1 - slot)
+                collect(j, j, False, False)
+                if j + AHEAD < tiles:
+                    score(j + AHEAD, j + AHEAD, keys)
+            return carry
+
+        rounds = 2 * chip
+        lax.fori_loop(0, rounds, sweep, 0)
+
+        def result(t):
+            scale = 1.0 / acc[t, HEAD_DIM:]
+            x = (bands(acc[t, :HEAD_DIM]) * scale[None]).reshape(HEAD_DIM, rows)
+            return x.T.astype(o_ref.dtype)
+
+        def give(h):
+            cols = head_cols(o * shared + h, HEAD_DIM)
+            return remote(stage.at[h], o_ref.at[:, cols], out_sem.at[0, h], out_sem.at[1, h], partner)
+
+        def take(h):
+            cols = head_cols((1 - o) * shared + h, HEAD_DIM)
+            return remote(stage.at[h], o_ref.at[:, cols], out_sem.at[0, h], out_sem.at[1, h], partner)
+
+        last = lax.rem(rounds + 1, 2)
+        for k in range(tiles - LAG, tiles):
+            weigh(k, k, last)
+            add(k - HOLD, k - HOLD, False)
+        for h in range(shared):
+            stage[h] = result(h)
+            if h >= 2:
+                give(h - 2).start()
+        for k in range(tiles - HOLD, tiles):
+            add(k, k, False)
+        for h in range(shared):
+            cols = head_cols(o * shared + h, HEAD_DIM)
+            o_ref[:, cols] = result(shared + h)
+            if h < 2:
+                give(shared - 2 + h).start()
+
+        def drain(r, carry):
+            _, _, _, early, onward = plan(r)
+            pl.when(early)(onward.wait_send)
+            return carry
+
+        lax.fori_loop(0, rounds, drain, 0)
+        for h in range(shared):
+            take(h).wait_recv()
+        for h in range(shared):
+            give(h).wait_send()
+        for wanted, copy in sends:
+            pl.when(wanted)(copy.wait_send)
+        give_q.wait_send()
+        give_kv.wait_send()
+
+    specs = [pltpu.ACC(m)((half, rows), f32) for m in range(2) for _ in range(4)]
+    specs += [pltpu.ACC(m)((n, rows), f32) for m in range(2) for _ in range(2) for n in (HEAD_DIM, SUMS)]
+    pl.run_scoped(pipeline, *specs)
+
+
+def paired(rows, width, shared):
+    half, tiles = rows // 2, 2 * shared
+    bf16, f32, dma = jnp.bfloat16, jnp.float32, pltpu.SemaphoreType.DMA
+    return pl.pallas_call(
+        functools.partial(paired_kernel, shared),
+        out_shape=pltpu.VMEM((rows, width), bf16),
+        in_specs=[pl.BlockSpec(memory_space=pltpu.HBM)] * 3,
+        out_specs=pl.BlockSpec(memory_space=pltpu.VMEM),
+        scratch_shapes=[
+            pltpu.VMEM((2, rows, shared * HEAD_DIM), bf16),
+            pltpu.VMEM((tiles, 2, 2 * HEAD_DIM, half), bf16),
+            pltpu.VMEM((8, 2, 2, half, HEAD_DIM), bf16),
+            pltpu.VMEM((2, 2, half, HEAD_DIM), bf16),
+            pltpu.VMEM((tiles, HEAD_DIM + 8, rows), f32),
+            pltpu.VMEM((tiles, 8, rows), f32),
+            pltpu.VMEM((tiles, 8, rows), f32),
+            pltpu.VMEM((RING, rows, rows), f32),
+            pltpu.VMEM((2, 2, HEAD_DIM + SUMS, half), bf16),
+            pltpu.VMEM((shared, rows, HEAD_DIM), bf16),
+            dma((9,)), dma((4,)), dma((2, 4)), dma((6,)), dma((8, 2)), dma((2, shared)),
+        ],
+        compiler_params=pltpu.CompilerParams(
+            collective_id=1, has_side_effects=True, vmem_limit_bytes=60 * 1024 * 1024))
+
+
 def solution(mesh):
     nc = mesh.shape["ctx"]
 
@@ -222,6 +518,8 @@
         per_dev = width // HEAD_DIM
         group = HEADS // KV_HEADS
         kv_dev = per_dev // min(group, per_dev)
+        if nc == 8 and kv_dev == 2 and rows == 2 * HEAD_DIM and per_dev == 2 * group:
+            return paired(rows, width, group)(queries, keys, values)
         any_space = pl.BlockSpec(memory_space=pltpu.HBM)
         return pl.pallas_call(
             functools.partial(kernel, nc, per_dev, group, kv_dev),

time: 20.3 us -> 18.4 us (0.906)
  Pallas kernels: 19.1 us -> 17.3 us
    pallas_call x1, Pallas kernels: 19.1 us -> 17.3 us  [step(): return paired(rows, width, group)(queries, keys, values)]
where the time goes in v1:
time: 18.4 us; the launch traced here: 18.2 us
  Pallas kernels  17.3 us (94%)
  local copies, waits for them, and re-layouts  0.97 us (5%)
    pallas_call x1, Pallas kernels, step(): return paired(rows, width, group)(queries, keys, values)  17.3 us
    unnamed x1, local copies, waits for them, and re-layouts  0.97 us

profile of v1, /device:TPU:29, one launch (start us, length us, event | category | flops | bytes accessed | tf_op | source)
XLA Modules:
  0.0 18.2 jit_solution(11067594335119965092)
XLA Ops:
  0.0 17.3 %shard_map.37 = bf16[256,2048]{1,0:T(8,128)(2,1)S(1)} custom-call(bf16[256,2048]{1,0:T(8,128)(2,1)} %q_hbm.1, bf16[256,1024]{1,0:T(8,128)(2,1)} %k_hbm.1, bf16[256,1024]{1,0:T(8,128)(2,1)} %v_hbm.1), custom_call_target="tpu_custom_call" | custom-call | tf_op jit(solution)/shard_map/pallas_call | solution.py:522
  17.3 1.0 %copy.5 = bf16[256,2048]{1,0:T(8,128)(2,1)} copy(bf16[256,2048]{1,0:T(8,128)(2,1)S(1)} %shard_map.37) | data formatting | bytes 2097152

commit v2 on v1

--- a/solution.py
+++ b/solution.py
@@ -219,6 +219,7 @@
 HOLD = 2
 RING = 8
 SUMS = 16
+PARTS = 2
 
 
 def paired_kernel(shared, q_hbm, k_hbm, v_hbm, o_ref, q_raw, q_t, kv, other, acc, peak, shrink,
@@ -413,7 +414,25 @@
             target = 2 * lax.select(chip == 3, 2, 3) + o
             return b1, b2, h, early, piece(b1, h, relay_sem.at[r], target)
 
-        def sweep(r, carry):
+        def result(t):
+            scale = 1.0 / acc[t, HEAD_DIM:]
+            x = (bands(acc[t, :HEAD_DIM]) * scale[None]).reshape(HEAD_DIM, rows)
+            return x.T.astype(o_ref.dtype)
+
+        def set_aside(h):
+            stage[:, h * HEAD_DIM:(h + 1) * HEAD_DIM] = result(h)
+
+        def keep(h):
+            o_ref[:, head_cols(o * shared + h, HEAD_DIM)] = result(shared + h)
+
+        part = shared // PARTS
+
+        def give(n, g):
+            cols = head_cols(g * PARTS + n, part * HEAD_DIM)
+            src = stage.at[:, n * part * HEAD_DIM:(n + 1) * part * HEAD_DIM]
+            return remote(src, o_ref.at[:, cols], out_sem.at[0, n], out_sem.at[1, n], partner)
+
+        def sweep(r, final):
             b1, b2, h, early, onward = plan(r)
             onward.wait_recv()
             pl.when(early)(onward.start)
@@ -431,39 +450,42 @@
                 collect(j, j, False, False)
                 if j + AHEAD < tiles:
                     score(j + AHEAD, j + AHEAD, keys)
+                if final and j >= LAG + HOLD:
+                    if n < shared:
+                        set_aside(n)
+                    else:
+                        keep(n - shared)
+                    if 0 < n <= shared and n % part == 0:
+                        give(n // part - 1, o).start()
+
+        rounds = 2 * chip
+
+        def body(r, carry):
+            sweep(r, False)
             return carry
 
-        rounds = 2 * chip
-        lax.fori_loop(0, rounds, sweep, 0)
-
-        def result(t):
-            scale = 1.0 / acc[t, HEAD_DIM:]
-            x = (bands(acc[t, :HEAD_DIM]) * scale[None]).reshape(HEAD_DIM, rows)
-            return x.T.astype(o_ref.dtype)
-
-        def give(h):
-            cols = head_cols(o * shared + h, HEAD_DIM)
-            return remote(stage.at[h], o_ref.at[:, cols], out_sem.at[0, h], out_sem.at[1, h], partner)
-
-        def take(h):
-            cols = head_cols((1 - o) * shared + h, HEAD_DIM)
-            return remote(stage.at[h], o_ref.at[:, cols], out_sem.at[0, h], out_sem.at[1, h], partner)
+        @pl.when(chip > 0)
+        def _():
+            lax.fori_loop(0, rounds - 1, body, 0)
+            sweep(rounds - 1, True)
+
+        @pl.when(chip == 0)
+        def _():
+            for h in range(shared):
+                set_aside(h)
+            for h in range(tiles - LAG - HOLD - shared):
+                keep(h)
+            for n in range(PARTS):
+                give(n, o).start()
 
         last = lax.rem(rounds + 1, 2)
         for k in range(tiles - LAG, tiles):
             weigh(k, k, last)
             add(k - HOLD, k - HOLD, False)
-        for h in range(shared):
-            stage[h] = result(h)
-            if h >= 2:
-                give(h - 2).start()
+            keep(k - HOLD - shared)
         for k in range(tiles - HOLD, tiles):
             add(k, k, False)
-        for h in range(shared):
-            cols = head_cols(o * shared + h, HEAD_DIM)
-            o_ref[:, cols] = result(shared + h)
-            if h < 2:
-                give(shared - 2 + h).start()
+            keep(k - shared)
 
         def drain(r, carry):
             _, _, _, early, onward = plan(r)
@@ -471,10 +493,9 @@
             return carry
 
         lax.fori_loop(0, rounds, drain, 0)
-        for h in range(shared):
-            take(h).wait_recv()
-        for h in range(shared):
-            give(h).wait_send()
+        for n in range(PARTS):
+            give(n, 1 - o).wait_recv()
+            give(n, o).wait_send()
         for wanted, copy in sends:
             pl.when(wanted)(copy.wait_send)
         give_q.wait_send()
@@ -503,8 +524,8 @@
             pltpu.VMEM((tiles, 8, rows), f32),
             pltpu.VMEM((RING, rows, rows), f32),
             pltpu.VMEM((2, 2, HEAD_DIM + SUMS, half), bf16),
-            pltpu.VMEM((shared, rows, HEAD_DIM), bf16),
-            dma((9,)), dma((4,)), dma((2, 4)), dma((6,)), dma((8, 2)), dma((2, shared)),
+            pltpu.VMEM((rows, shared * HEAD_DIM), bf16),
+            dma((9,)), dma((4,)), dma((2, 4)), dma((6,)), dma((8, 2)), dma((2, PARTS)),
         ],
         compiler_params=pltpu.CompilerParams(
             collective_id=1, has_side_effects=True, vmem_limit_bytes=60 * 1024 * 1024))

time: 18.4 us -> 17.7 us (0.962)
  Pallas kernels: 17.3 us -> 16.6 us
    pallas_call x1, Pallas kernels: 17.3 us -> 16.6 us  [step(): return paired(rows, width, group)(queries, keys, values)]
where the time goes in v2:
time: 17.7 us; the launch traced here: 17.6 us
  Pallas kernels  16.6 us (94%)
  local copies, waits for them, and re-layouts  0.97 us (5%)
    pallas_call x1, Pallas kernels, step(): return paired(rows, width, group)(queries, keys, values)  16.6 us
    unnamed x1, local copies, waits for them, and re-layouts  0.97 us

profile of v2, /device:TPU:29, one launch (start us, length us, event | category | flops | bytes accessed | tf_op | source)
XLA Modules:
  0.0 17.6 jit_solution(6646389958245725924)
XLA Ops:
  0.0 16.6 %shard_map.37 = bf16[256,2048]{1,0:T(8,128)(2,1)S(1)} custom-call(bf16[256,2048]{1,0:T(8,128)(2,1)} %q_hbm.1, bf16[256,1024]{1,0:T(8,128)(2,1)} %k_hbm.1, bf16[256,1024]{1,0:T(8,128)(2,1)} %v_hbm.1), custom_call_target="tpu_custom_call" | custom-call | tf_op jit(solution)/shard_map/pallas_call | solution.py:543
  16.6 1.0 %copy.5 = bf16[256,2048]{1,0:T(8,128)(2,1)} copy(bf16[256,2048]{1,0:T(8,128)(2,1)S(1)} %shard_map.37) | data formatting | bytes 2097152

commit v3 on v2

--- a/solution.py
+++ b/solution.py
@@ -220,6 +220,7 @@
 RING = 8
 SUMS = 16
 PARTS = 2
+LATE = 2
 
 
 def paired_kernel(shared, q_hbm, k_hbm, v_hbm, o_ref, q_raw, q_t, kv, other, acc, peak, shrink,
@@ -254,8 +255,16 @@
     across = 2 * lax.rem(chip + 2, 4)
     for target in (partner, beside, beside + 1, across, across + 1):
         pl.semaphore_signal(barrier, inc=1, device_id={"ctx": target})
+    middle = (chip == 1) | (chip == 2)
+    opposite = 2 * (3 - chip)
+
+    @pl.when(middle)
+    def _():
+        for target in (opposite, opposite + 1):
+            pl.semaphore_signal(barrier, inc=1, device_id={"ctx": target})
+
     v_t[...] = jnp.ones(v_t.shape, bf16)
-    pl.semaphore_wait(barrier, 5)
+    pl.semaphore_wait(barrier, lax.select(middle, 7, 5))
 
     def remote(src, dst, send, recv, target):
         return pltpu.make_async_remote_copy(
@@ -285,6 +294,15 @@
     for wanted, copy in sends:
         pl.when(wanted)(copy.start)
     give_kv.start()
+    late = [remote(other.at[1], kv.at[c, 1], send_sem.at[2, 1], recv_sem.at[c, 1], opposite + 1 - o)]
+    sends += [(chip == 1, copy) for copy in late]
+
+    def send_late():
+        for copy in late:
+            pl.when(chip == 1)(copy.start)
+
+    if LATE == 0:
+        send_late()
 
     def prepare(slot):
         for h in range(shared):
@@ -360,20 +378,22 @@
             acc[t, HEAD_DIM:] = total
 
         pairs = lambda b: ((b, 0), (b, 1))
-        late = o * shared
+        lower = o * shared
         jobs = []
         for h in range(shared):
             jobs.append((shared + h, pairs(c), 0, True, True))
         for h in range(shared):
             jobs.append((h, pairs(partner), 1, True, True))
         for h in range(shared):
-            jobs.append((late + h, pairs(2 * chip), o, False, False))
+            jobs.append((lower + h, pairs(2 * chip), o, False, False))
 
         load_q.wait()
         prepare(1)
         turn(0, c, 0, c, 1)
 
         def meet():
+            if LATE == 1:
+                send_late()
             give_kv.wait_recv()
             give_q.wait_recv()
             prepare(0)
@@ -412,7 +432,8 @@
                                                          lax.select(early, 4 + e, 1)))
             h = lax.select(chip == 3, lax.select(early, r // 2, r - 4), lax.rem(r, 2))
             target = 2 * lax.select(chip == 3, 2, 3) + o
-            return b1, b2, h, early, piece(b1, h, relay_sem.at[r], target)
+            onward = early & (r < 3)
+            return b1, b2, h, onward, piece(b1, h, relay_sem.at[r], target)
 
         def result(t):
             scale = 1.0 / acc[t, HEAD_DIM:]
@@ -458,6 +479,8 @@
                     if 0 < n <= shared and n % part == 0:
                         give(n // part - 1, o).start()
 
+        if LATE == 2:
+            send_late()
         rounds = 2 * chip
 
         def body(r, carry):
@@ -525,7 +548,7 @@
             pltpu.VMEM((RING, rows, rows), f32),
             pltpu.VMEM((2, 2, HEAD_DIM + SUMS, half), bf16),
             pltpu.VMEM((rows, shared * HEAD_DIM), bf16),
-            dma((9,)), dma((4,)), dma((2, 4)), dma((6,)), dma((8, 2)), dma((2, PARTS)),
+            dma((9,)), dma((4,)), dma((3, 4)), dma((6,)), dma((8, 2)), dma((2, PARTS)),
         ],
         compiler_params=pltpu.CompilerParams(
             collective_id=1, has_side_effects=True, vmem_limit_bytes=60 * 1024 * 1024))

time: 17.7 us -> 17.1 us (0.966)
  Pallas kernels: 16.6 us -> 16 us
    pallas_call x1, Pallas kernels: 16.6 us -> 16 us  [step(): return paired(rows, width, group)(queries, keys, values)]
where the time goes in v3:
time: 17.1 us; the launch traced here: 17 us
  Pallas kernels  16 us (94%)
  local copies, waits for them, and re-layouts  0.97 us (6%)
    pallas_call x1, Pallas kernels, step(): return paired(rows, width, group)(queries, keys, values)  16 us
    unnamed x1, local copies, waits for them, and re-layouts  0.97 us

profile of v3, /device:TPU:29, one launch (start us, length us, event | category | flops | bytes accessed | tf_op | source)
XLA Modules:
  0.0 17.0 jit_solution(15198644722372559321)
XLA Ops:
  0.0 16.0 %shard_map.37 = bf16[256,2048]{1,0:T(8,128)(2,1)S(1)} custom-call(bf16[256,2048]{1,0:T(8,128)(2,1)} %q_hbm.1, bf16[256,1024]{1,0:T(8,128)(2,1)} %k_hbm.1, bf16[256,1024]{1,0:T(8,128)(2,1)} %v_hbm.1), custom_call_target="tpu_custom_call" | custom-call | tf_op jit(solution)/shard_map/pallas_call | solution.py:566
  16.0 1.0 %copy.5 = bf16[256,2048]{1,0:T(8,128)(2,1)} copy(bf16[256,2048]{1,0:T(8,128)(2,1)S(1)} %shard_map.37) | data formatting | bytes 2097152

commit v4 on v3

--- a/solution.py
+++ b/solution.py
@@ -215,12 +215,11 @@
 
 
 AHEAD = 4
-LAG = 4
+LAG = 3
 HOLD = 2
 RING = 8
 SUMS = 16
-PARTS = 2
-LATE = 2
+ENDS = (4, 7, 8)
 
 
 def paired_kernel(shared, q_hbm, k_hbm, v_hbm, o_ref, q_raw, q_t, kv, other, acc, peak, shrink,
@@ -301,9 +300,6 @@
         for copy in late:
             pl.when(chip == 1)(copy.start)
 
-    if LATE == 0:
-        send_late()
-
     def prepare(slot):
         for h in range(shared):
             x = q_raw[slot, :, h * HEAD_DIM:(h + 1) * HEAD_DIM].astype(f32) * EXP2_SCALE
@@ -392,8 +388,6 @@
         turn(0, c, 0, c, 1)
 
         def meet():
-            if LATE == 1:
-                send_late()
             give_kv.wait_recv()
             give_q.wait_recv()
             prepare(0)
@@ -446,11 +440,14 @@
         def keep(h):
             o_ref[:, head_cols(o * shared + h, HEAD_DIM)] = result(shared + h)
 
-        part = shared // PARTS
+        ends = [shared * x // 8 for x in ENDS]
+        begins = [0] + ends[:-1]
 
         def give(n, g):
-            cols = head_cols(g * PARTS + n, part * HEAD_DIM)
-            src = stage.at[:, n * part * HEAD_DIM:(n + 1) * part * HEAD_DIM]
+            width = (ends[n] - begins[n]) * HEAD_DIM
+            lo = begins[n] * HEAD_DIM
+            cols = pl.ds(pl.multiple_of(g * span + lo, HEAD_DIM), width)
+            src = stage.at[:, lo:lo + width]
             return remote(src, o_ref.at[:, cols], out_sem.at[0, n], out_sem.at[1, n], partner)
 
         def sweep(r, final):
@@ -476,11 +473,10 @@
                         set_aside(n)
                     else:
                         keep(n - shared)
-                    if 0 < n <= shared and n % part == 0:
-                        give(n // part - 1, o).start()
-
-        if LATE == 2:
-            send_late()
+                    if n + 1 in ends:
+                        give(ends.index(n + 1), o).start()
+
+        send_late()
         rounds = 2 * chip
 
         def body(r, carry):
@@ -498,7 +494,7 @@
                 set_aside(h)
             for h in range(tiles - LAG - HOLD - shared):
                 keep(h)
-            for n in range(PARTS):
+            for n in range(len(ENDS)):
                 give(n, o).start()
 
         last = lax.rem(rounds + 1, 2)
@@ -516,7 +512,7 @@
             return carry
 
         lax.fori_loop(0, rounds, drain, 0)
-        for n in range(PARTS):
+        for n in range(len(ENDS)):
             give(n, 1 - o).wait_recv()
             give(n, o).wait_send()
         for wanted, copy in sends:
@@ -548,7 +544,7 @@
             pltpu.VMEM((RING, rows, rows), f32),
             pltpu.VMEM((2, 2, HEAD_DIM + SUMS, half), bf16),
             pltpu.VMEM((rows, shared * HEAD_DIM), bf16),
-            dma((9,)), dma((4,)), dma((3, 4)), dma((6,)), dma((8, 2)), dma((2, PARTS)),
+            dma((9,)), dma((4,)), dma((3, 4)), dma((6,)), dma((8, 2)), dma((2, len(ENDS))),
         ],
         compiler_params=pltpu.CompilerParams(
             collective_id=1, has_side_effects=True, vmem_limit_bytes=60 * 1024 * 1024))

time: 17.1 us -> 16.7 us (0.977)
  Pallas kernels: 16 us -> 15.6 us
    pallas_call x1, Pallas kernels: 16 us -> 15.6 us  [step(): return paired(rows, width, group)(queries, keys, values)]
where the time goes in v4:
time: 16.7 us; the launch traced here: 16.6 us
  Pallas kernels  15.6 us (93%)
  local copies, waits for them, and re-layouts  0.97 us (6%)
    pallas_call x1, Pallas kernels, step(): return paired(rows, width, group)(queries, keys, values)  15.6 us
    unnamed x1, local copies, waits for them, and re-layouts  0.97 us

profile of v4, /device:TPU:29, one launch (start us, length us, event | category | flops | bytes accessed | tf_op | source)
XLA Modules:
  0.0 16.6 jit_solution(11517485435824656117)
XLA Ops:
  0.0 15.6 %shard_map.37 = bf16[256,2048]{1,0:T(8,128)(2,1)S(1)} custom-call(bf16[256,2048]{1,0:T(8,128)(2,1)} %q_hbm.1, bf16[256,1024]{1,0:T(8,128)(2,1)} %k_hbm.1, bf16[256,1024]{1,0:T(8,128)(2,1)} %v_hbm.1), custom_call_target="tpu_custom_call" | custom-call | tf_op jit(solution)/shard_map/pallas_call | solution.py:562
  15.6 1.0 %copy.5 = bf16[256,2048]{1,0:T(8,128)(2,1)} copy(bf16[256,2048]{1,0:T(8,128)(2,1)S(1)} %shard_map.37) | data formatting | bytes 2097152

commit v5 on v4

--- a/solution.py
+++ b/solution.py
@@ -244,11 +244,6 @@
             for n, (g, dst) in enumerate(((o, kv.at[c, h, i]), (1 - o, other.at[h, i]))):
                 src = ref.at[pl.ds(h * half, half), head_cols(2 * tp + g, HEAD_DIM)]
                 loads.append(pltpu.make_async_copy(src, dst, load_sem.at[4 * h + 2 * i + n]))
-    for load in loads:
-        load.start()
-    load_q = pltpu.make_async_copy(q_hbm.at[:, head_cols(o, span)], q_raw.at[1], load_sem.at[8])
-    load_q.start()
-
     barrier = pltpu.get_barrier_semaphore()
     beside = 2 * (chip + 1 - 2 * lax.rem(chip, 2))
     across = 2 * lax.rem(chip + 2, 4)
@@ -262,6 +257,11 @@
         for target in (opposite, opposite + 1):
             pl.semaphore_signal(barrier, inc=1, device_id={"ctx": target})
 
+    for load in loads:
+        load.start()
+    load_q = pltpu.make_async_copy(q_hbm.at[:, head_cols(o, span)], q_raw.at[1], load_sem.at[8])
+    load_q.start()
+
     v_t[...] = jnp.ones(v_t.shape, bf16)
     pl.semaphore_wait(barrier, lax.select(middle, 7, 5))
 
@@ -274,7 +274,6 @@
 
     give_q = remote(q_hbm.at[:, head_cols(1 - o, span)], q_raw.at[0], pair_sem.at[0], pair_sem.at[1], partner)
     give_kv = remote(other, kv.at[c], pair_sem.at[2], pair_sem.at[3], partner)
-    give_q.start()
     for load in loads:
         load.wait()
     sends = []
@@ -292,6 +291,7 @@
                 sends.append((wanted, (same, cross)[swap]))
     for wanted, copy in sends:
         pl.when(wanted)(copy.start)
+    give_q.start()
     give_kv.start()
     late = [remote(other.at[1], kv.at[c, 1], send_sem.at[2, 1], recv_sem.at[c, 1], opposite + 1 - o)]
     sends += [(chip == 1, copy) for copy in late]
@@ -463,8 +463,8 @@
             for j in range(tiles):
                 k = (j - LAG) % tiles
                 n = (j - LAG - HOLD) % tiles
+                weigh(k, k, slot if j >= LAG else 1 - slot)
                 add(n, n, False)
-                weigh(k, k, slot if j >= LAG else 1 - slot)
                 collect(j, j, False, False)
                 if j + AHEAD < tiles:
                     score(j + AHEAD, j + AHEAD, keys)
@@ -476,7 +476,6 @@
                     if n + 1 in ends:
                         give(ends.index(n + 1), o).start()
 
-        send_late()
         rounds = 2 * chip
 
         def body(r, carry):
@@ -486,6 +485,7 @@
         @pl.when(chip > 0)
         def _():
             lax.fori_loop(0, rounds - 1, body, 0)
+            send_late()
             sweep(rounds - 1, True)
 
         @pl.when(chip == 0)

time: 16.7 us -> 16.2 us (0.970)
  Pallas kernels: 15.6 us -> 14.9 us
    pallas_call x1, Pallas kernels: 15.6 us -> 14.9 us  [step(): return paired(rows, width, group)(queries, keys, values)]
where the time goes in v5:
time: 16.2 us; the launch traced here: 15.9 us
  Pallas kernels  14.9 us (92%)
  local copies, waits for them, and re-layouts  0.97 us (6%)
    pallas_call x1, Pallas kernels, step(): return paired(rows, width, group)(queries, keys, values)  14.9 us
    unnamed x1, local copies, waits for them, and re-layouts  0.97 us

profile of v5, /device:TPU:29, one launch (start us, length us, event | category | flops | bytes accessed | tf_op | source)
XLA Modules:
  0.0 15.9 jit_solution(13655177935841031071)
XLA Ops:
  0.0 14.9 %shard_map.37 = bf16[256,2048]{1,0:T(8,128)(2,1)S(1)} custom-call(bf16[256,2048]{1,0:T(8,128)(2,1)} %q_hbm.1, bf16[256,1024]{1,0:T(8,128)(2,1)} %k_hbm.1, bf16[256,1024]{1,0:T(8,128)(2,1)} %v_hbm.1), custom_call_target="tpu_custom_call" | custom-call | tf_op jit(solution)/shard_map/pallas_call | solution.py:562
  15.0 1.0 %copy.5 = bf16[256,2048]{1,0:T(8,128)(2,1)} copy(bf16[256,2048]{1,0:T(8,128)(2,1)S(1)} %shard_map.37) | data formatting | bytes 2097152

commit v6 on v5

--- a/solution.py
+++ b/solution.py
@@ -216,7 +216,7 @@
 
 AHEAD = 4
 LAG = 3
-HOLD = 2
+HOLD = 3
 RING = 8
 SUMS = 16
 ENDS = (4, 7, 8)

time: 16.2 us -> 16.2 us (level)
  no operation moved by 1% of the time
where the time goes in v6:
time: 16.2 us; the launch traced here: 15.9 us
  Pallas kernels  15 us (93%)
  local copies, waits for them, and re-layouts  0.97 us (6%)
    pallas_call x1, Pallas kernels, step(): return paired(rows, width, group)(queries, keys, values)  15 us
    unnamed x1, local copies, waits for them, and re-layouts  0.97 us

profile of v6, /device:TPU:29, one launch (start us, length us, event | category | flops | bytes accessed | tf_op | source)
XLA Modules:
  0.0 15.9 jit_solution(8419420353843300718)
XLA Ops:
  0.0 15.0 %shard_map.37 = bf16[256,2048]{1,0:T(8,128)(2,1)S(1)} custom-call(bf16[256,2048]{1,0:T(8,128)(2,1)} %q_hbm.1, bf16[256,1024]{1,0:T(8,128)(2,1)} %k_hbm.1, bf16[256,1024]{1,0:T(8,128)(2,1)} %v_hbm.1), custom_call_target="tpu_custom_call" | custom-call | tf_op jit(solution)/shard_map/pallas_call | solution.py:562
  15.0 1.0 %copy.5 = bf16[256,2048]{1,0:T(8,128)(2,1)} copy(bf16[256,2048]{1,0:T(8,128)(2,1)S(1)} %shard_map.37) | data formatting | bytes 2097152
